TPU v7x, 32 devices: a whole 2x2x4 slice. The times are simulated.
32 devices in a mesh: dp: 4 (over z), tp: 8 (over y, x, core).
Axes of the slice: x: 2, y: 2, z: 4, core: 2. Of those that a mesh axis runs over, the one named last changes fastest.
Arguments:
- hidden: bfloat16 [2048, 640], P(('dp', 'tp'))
- w_unembed: bfloat16 [640, 262144], P(('dp', 'tp'))
Outputs:
- output: bfloat16 [2048, 262144], P(None, ('dp', 'tp'))
All inputs are finite; a program needn't handle non-finite values.
Results may differ from a plain program's by a relative error of at most 0.001.
Values are sent between devices in bfloat16 or wider.
A program may use at most 1 GiB of HBM per device.

v0:
```python
import jax
import jax.numpy as jnp
from jax import lax
from jax.sharding import PartitionSpec as P, NamedSharding


def solution(mesh):
    outer_size = mesh.shape["dp"]
    inner_size = mesh.shape["tp"]

    def local_part(hid_blk, w_blk):
        full_hidden = lax.all_gather(hid_blk, ("dp", "tp"), axis=0, tiled=True)
        rows_loc, vocab_size = w_blk.shape
        col_width = vocab_size // (outer_size * inner_size)
        w_split = w_blk.reshape(rows_loc, outer_size, inner_size, col_width)
        w_step = lax.all_to_all(w_split, "tp", 2, 0, tiled=True)
        w_cols = lax.all_to_all(w_step, "dp", 1, 0, tiled=True)
        w_cols = w_cols.reshape(outer_size * inner_size * rows_loc, col_width)
        return jnp.dot(full_hidden, w_cols, preferred_element_type=jnp.float32).astype(jnp.bfloat16)

    return jax.shard_map(
        local_part,
        mesh=mesh,
        in_specs=(P(("dp", "tp"), None), P(("dp", "tp"), None)),
        out_specs=P(None, ("dp", "tp")),
        check_vma=False,
    )
```

profile of v0, /device:TPU:0, one launch (start us, length us, event | category | flops | bytes accessed | tf_op | source)
XLA Modules:
  0.0 465.0 jit_solution(9367104241878155000)
XLA Ops:
  6.5 14.4 %copy.7 = bf16[3,8,32,8192]{3,2,1,0:T(8,128)(2,1)} copy(bf16[3,8,32,8192]{3,1,2,0:T(8,128)(2,1)} %bitcast.19) | data formatting | bytes 25165824
  20.9 9.2 %slice_bitcast_fusion = bf16[20,4,8,8192]{3,2,1,0:T(8,128)(2,1)} fusion(bf16[24,32,8192]{2,1,0:T(8,128)(2,1)} %bitcast.17), kind=kLoop, calls=%fused_computation.1 | loop fusion | bytes 20971520 | tf_op jit(solution)/shard_map/reshape | solution.py:15
  30.2 12.2 %copy.5 = bf16[20,4,8,8192]{3,1,0,2:T(4,128)(2,1)S(1)} copy(bf16[20,4,8,8192]{3,2,1,0:T(8,128)(2,1)} %slice_bitcast_fusion) | data formatting | bytes 20971520 | tf_op jit(solution)/shard_map/reshape | solution.py:15
  42.4 121.5 %all_to_all.33 = bf16[20,4,8,8192]{3,1,0,2:T(4,128)(2,1)} all-to-all(bf16[20,4,8,8192]{3,1,0,2:T(4,128)(2,1)S(1)} %copy.5), channel_id=1, replica_groups=mesh['dp'=4,'tp'=8] {'tp'}, dimensions={2} | all-to-all | bytes 20971520 | tf_op jit(solution)/shard_map/all_to_all | solution.py:16
  163.9 13.8 %copy.6 = bf16[160,4,1,8192]{3,0,2,1:T(8,128)(2,1)} copy(bf16[160,4,1,8192]{3,1,0,2:T(4,128)(2,1)} %bitcast.18) | data formatting | bytes 20971520 | tf_op jit(solution)/shard_map/all_to_all | solution.py:16
  177.7 6.0 %all-to-all-start.1 = ((bf16[160,4,1,8192]{3,0,2,1:T(8,128)(2,1)}), bf16[160,4,1,8192]{3,0,2,1:T(8,128)(2,1)}, u32[]{:S(2)}, u32[]{:S(2)}) async-start(bf16[160,4,1,8192]{3,0,2,1:T(8,128)(2,1)} %copy.6), calls=%async_computation.1 | async-start | bytes 20971520 | tf_op jit(solution)/shard_map/all_to_all | solution.py:17
  183.7 0.2 all-gather.2.cloned.1.call-start
  183.9 0.5 all-gather.2.cloned.1.call-update
  184.4 198.8 %all-gather.2.cloned.1.call-done = bf16[2048,640]{1,0:T(8,128)(2,1)} async-done(((bf16[64,640]{1,0:T(8,128)(2,1)}), bf16[2048,640]{1,0:T(8,128)(2,1)}) %all-gather.2.cloned.1.call-update) | async-done | bytes 2621456 | tf_op jit(solution)/shard_map/all_gather | solution.py:12
  383.2 40.5 %all-to-all-done.1 = bf16[160,4,1,8192]{3,0,2,1:T(8,128)(2,1)} async-done(((bf16[160,4,1,8192]{3,0,2,1:T(8,128)(2,1)}), bf16[160,4,1,8192]{3,0,2,1:T(8,128)(2,1)}, u32[]{:S(2)}, u32[]{:S(2)}) %all-to-all-start.1) | async-done | bytes 10485792 | tf_op jit(solution)/shard_map/all_to_all | solution.py:17
  423.7 34.4 %convolution_convert_fusion = bf16[2048,8192]{1,0:T(8,128)(2,1)} fusion(bf16[2048,640]{1,0:T(8,128)(2,1)} %all-gather.2.cloned.1.call-done, bf16[640,8192]{1,0:T(8,128)(2,1)} %bitcast.5), kind=kOutput, calls=%fused_computation | convolution fusion | flops 21491613696 | bytes 46661632 | tf_op jit(solution)/shard_map/dot_general | solution.py:19
Async XLA Ops:
  177.7 246.0 %all-to-all-start.1 = ((bf16[160,4,1,8192]{3,0,2,1:T(8,128)(2,1)}), bf16[160,4,1,8192]{3,0,2,1:T(8,128)(2,1)}, u32[]{:S(2)}, u32[]{:S(2)}) async-start(bf16[160,4,1,8192]{3,0,2,1:T(8,128)(2,1)} %copy.6), calls=%async_computation.1 | async-start | bytes 20971520 | tf_op jit(solution)/shard_map/all_to_all | solution.py:17
  183.7 199.5 %all-gather.2.cloned.1.call-start = ((), (), s32[]{:S(2)}) async-start(), calls=%async_computation.2 | async-start | bytes 2703360 | tf_op jit(solution)/shard_map/all_gather | solution.py:12
Sparse Core Ops, SparseCore 0:
  187.3 195.8 all-gather.1
where the time goes:
time: 465 us
  waiting for transfers between devices  240 us (52%)
  blocking collectives  121 us (26%)
  local copies, waits for them, and re-layouts  49.7 us (11%)
  matrix products  34.4 us (7%)
  between operations  13.4 us (3%)
  starting transfers between devices  6.21 us (1%)
    all_gather x1, waiting for transfers between devices, local_part(): full_hidden = lax.all_gather(hid_blk, ('dp', 'tp'), axis=0, tiled=True)  199 us
    all_to_all x1, blocking collectives, local_part(): w_step = lax.all_to_all(w_split, 'tp', 2, 0, tiled=True)  121 us
    all_to_all x1, waiting for transfers between devices, local_part(): w_cols = lax.all_to_all(w_step, 'dp', 1, 0, tiled=True)  40.5 us
    dot_general x1, matrix products, local_part(): jnp.dot(full_hidden, w_cols, preferred_element_type=jnp.float32)  34.4 us
    reshape x2, local copies, waits for them, and re-layouts, local_part(): w_split = w_blk.reshape(rows_loc, outer_size, inner_size, col_width)  21.4 us
    unnamed x1, local copies, waits for them, and re-layouts  14.4 us
    all_to_all x1, local copies, waits for them, and re-layouts, local_part(): w_step = lax.all_to_all(w_split, 'tp', 2, 0, tiled=True)  13.8 us
  transfers between devices with their start and end apart: 2, of which 2 were waited for; matrix products, arithmetic and copies ran while one was open for 0% of the time, Pallas kernels for 0%

commit v1 on v0

v1 whole, which is shorter than its diff:
```python
import functools, jax, jax.numpy as jnp
from jax import lax
from jax.experimental import pallas as pl
from jax.experimental.pallas import tpu as pltpu
from jax.sharding import PartitionSpec as P

def mm(h_ref, a1, a2, b, y_in, y_ref):
    nb = pl.program_id(0)
    del y_in
    acc = jnp.dot(h_ref[:, 0:256], a1[...], preferred_element_type=jnp.float32)
    acc += jnp.dot(h_ref[:, 256:512], a2[...], preferred_element_type=jnp.float32)
    half = (nb * 2) // pl.num_programs(0)
    off = pl.multiple_of(512 + half * 256, 256)
    acc += jnp.dot(h_ref[:, pl.ds(off, 256)], b[...], preferred_element_type=jnp.float32)
    y_ref[...] = acc.astype(jnp.bfloat16)

def chunk_mm(h4, r, y, c, nc, tn=512, M=2048):
    nt = nc // tn
    specs = [pl.BlockSpec((M, 1024), lambda j: (0, 0)),
             pl.BlockSpec((256, tn), lambda j: (0, j)),
             pl.BlockSpec((256, tn), lambda j: (0, nt + j)),
             pl.BlockSpec((256, tn), lambda j: (0, 2 * nt + j % (nt // 2)))]
    kw = {}
    args = (h4, r, r, r)
    if y is not None:
        specs.append(pl.BlockSpec(memory_space=pl.ANY)); args += (y,); kw = dict(input_output_aliases={4: 0})
        body = mm
    else:
        body = lambda h, a1, a2, b, o: mm(h, a1, a2, b, None, o)
    return pl.pallas_call(body, grid=(nt,), out_shape=jax.ShapeDtypeStruct((2048, 8192), jnp.bfloat16),
        in_specs=specs, out_specs=pl.BlockSpec((M, tn), lambda j: (0, c * nt + j)),
        cost_estimate=pl.CostEstimate(flops=2*2048*768*nc, bytes_accessed=2048*nc*2, transcendentals=0),
        compiler_params=pltpu.CompilerParams(dimension_semantics=("arbitrary",), vmem_limit_bytes=50*2**20), **kw)(*args)

NCH = 1
def solution(mesh):
    def f(h, w):
        n = 32
        H = lax.all_gather(h, ("dp", "tp"), axis=0, tiled=True)
        h3 = H.reshape(2048, 32, 20)
        z = jnp.zeros((2048, 32, 4), jnp.bfloat16)
        h4 = jnp.concatenate([h3[:, :, 0:8].reshape(2048, 256), h3[:, :, 8:16].reshape(2048, 256),
             jnp.concatenate([h3[:, :, 16:], z], 2).reshape(2048, 256),
             jnp.concatenate([z, h3[:, :, 16:]], 2).reshape(2048, 256)], 1)
        nc = 8192 // NCH
        w3 = w.reshape(20, n, NCH, nc)
        y = None
        for c in range(NCH):
            x = w3[:, :, c]
            a1 = x[0:8].transpose(1, 0, 2); a2 = x[8:16].transpose(1, 0, 2)
            b = x[16:].reshape(4, n, 2, nc // 2).transpose(1, 2, 0, 3).reshape(n, 8, nc // 2)
            p = jnp.concatenate([a1, a2, b], 2)
            r = lax.all_to_all(p, ("dp", "tp"), 0, 0, tiled=True).reshape(256, nc * 5 // 2)
            y = chunk_mm(h4, r, y, c, nc)
        return y
    return jax.shard_map(f, mesh=mesh, in_specs=(P(("dp", "tp"), None), P(("dp", "tp"), None)),
        out_specs=P(None, ("dp", "tp")), check_vma=False)
```

time: 465 us -> 323 us (0.69); the launches traced: 465 us -> 317 us
  blocking collectives: 121 us -> 0 us
  matrix products: 34.4 us -> 0 us
  Pallas kernels: 0 us -> 33.5 us
  waiting for transfers between devices: 240 us -> 214 us
  local copies, waits for them, and re-layouts: 49.7 us -> 34.6 us
  other arithmetic: 0 us -> 14.2 us
    all_to_all x1 -> x0, blocking collectives: 121 us -> none  [local_part(): w_step = lax.all_to_all(w_split, 'tp', 2, 0, tiled=True)]
    all_gather x1, waiting for transfers between devices: 199 us -> 94.4 us  [f(): H = lax.all_gather(h, ('dp', 'tp'), axis=0, tiled=True)]
    all_to_all x1, waiting for transfers between devices: 40.5 us -> 119 us  [f(): lax.all_to_all(p, ('dp', 'tp'), 0, 0, tiled=True).reshape(256, nc * 5 // 2)]
    dot_general x1 -> x0, matrix products: 34.4 us -> none  [local_part(): jnp.dot(full_hidden, w_cols, preferred_element_type=jnp.float32)]
    pallas_call x0 -> x1, Pallas kernels: none -> 33.5 us  [chunk_mm(): pl.pallas_call(body, grid=(nt,), out_shape=jax.ShapeDtypeStruct((2048, 81...]
    unnamed x1 -> x0, local copies, waits for them, and re-layouts: 14.4 us -> none
    concatenate x0 -> x2, other arithmetic: none -> 14.2 us  [the longest x1 10.6 us: f(): p = jnp.concatenate([a1, a2, b], 2)]
    all_to_all x1 -> x0, local copies, waits for them, and re-layouts: 13.8 us -> none  [local_part(): w_step = lax.all_to_all(w_split, 'tp', 2, 0, tiled=True)]
  transfers between devices with their start and end apart: 2 -> 2, of which waited for: 2 -> 2; matrix products, arithmetic and copies ran while one was open for 0% -> 7% of each run, Pallas kernels for 0% -> 0%
where the time goes in v1:
time: 323 us; the launch traced here: 317 us
  waiting for transfers between devices  214 us (66%)
  local copies, waits for them, and re-layouts  34.6 us (11%)
  Pallas kernels  33.5 us (10%)
  other arithmetic  14.2 us (4%)
  between operations  13.5 us (4%)
  starting transfers between devices  7.51 us (2%)
    all_to_all x1, waiting for transfers between devices, f(): lax.all_to_all(p, ('dp', 'tp'), 0, 0, tiled=True).reshape(256, nc * 5 // 2)  119 us
    all_gather x1, waiting for transfers between devices, f(): H = lax.all_gather(h, ('dp', 'tp'), axis=0, tiled=True)  94.4 us
    pallas_call x1, Pallas kernels, chunk_mm(): pl.pallas_call(body, grid=(nt,), out_shape=jax.ShapeDtypeStruct((2048, 81...  33.5 us
    concatenate x1, other arithmetic, f(): p = jnp.concatenate([a1, a2, b], 2)  10.6 us
    all_to_all x1, starting transfers between devices, f(): lax.all_to_all(p, ('dp', 'tp'), 0, 0, tiled=True).reshape(256, nc * 5 // 2)  7.47 us
  transfers between devices with their start and end apart: 2, of which 2 were waited for; matrix products, arithmetic and copies ran while one was open for 7% of the time, Pallas kernels for 0%

profile of v1, /device:TPU:0, one launch (start us, length us, event | category | flops | bytes accessed | tf_op | source)
XLA Modules:
  0.0 317.1 jit_solution(6143735832916926231)
XLA Ops:
  6.5 0.0 slice-start
  6.5 5.9 %fusion = (bf16[8,262144]{1,0:T(8,128)(2,1)}, bf16[8,262144]{1,0:T(8,128)(2,1)}) fusion(bf16[20,262144]{1,0:T(8,128)(2,1)} %param.3), kind=kLoop, calls=%fused_computation.6 | loop fusion | bytes 16777216 | tf_op jit(solution)/shard_map/slice | solution.py:50
  12.4 0.0 slice-done
  12.4 3.4 %reshape.33 = bf16[4,32,2,4096]{3,2,1,0:T(2,128)(2,1)} reshape(bf16[4,262144]{1,0:T(4,128)(2,1)S(1)} %slice-done) | data formatting | bytes 4194304 | tf_op jit(solution)/shard_map/reshape | solution.py:51
  15.8 4.9 %copy.9 = bf16[32,2,4,4096]{3,2,1,0:T(4,128)(2,1)} copy(bf16[32,2,4,4096]{3,1,0,2:T(2,128)(2,1)} %bitcast.20) | data formatting | bytes 4194304 | tf_op jit(solution)/shard_map/transpose | solution.py:51
  20.7 2.5 reshape.34
  23.3 10.6 %pad_maximum_fusion = bf16[32,8,20480]{2,1,0:T(8,128)(2,1)} fusion(bf16[32,8,4096]{2,1,0:T(8,128)(2,1)S(1)} %reshape.34, bf16[32,8,8192]{2,1,0:T(8,128)(2,1)} %bitcast.19, bf16[32,8,8192]{2,1,0:T(8,128)(2,1)} %bitcast.18), kind=kLoop, calls=%fused_computation | loop fusion | flops 31457280 | bytes 20971520 | tf_op jit(solution)/shard_map/concatenate | solution.py:52
  33.9 7.5 %all-to-all-start = ((bf16[32,8,20480]{2,1,0:T(8,128)(2,1)}), bf16[32,8,20480]{2,1,0:T(8,128)(2,1)}, u32[]{:S(2)}, u32[]{:S(2)}) async-start(bf16[32,8,20480]{2,1,0:T(8,128)(2,1)} %pad_maximum_fusion), calls=%async_computation | async-start | bytes 20971520 | tf_op jit(solution)/shard_map/all_to_all | solution.py:53
  41.4 0.0 all-gather.2.cloned.1.call-start
  41.5 0.7 all-gather.2.cloned.1.call-update
  42.1 94.4 %all-gather.2.cloned.1.call-done = bf16[2048,640]{1,0:T(8,128)(2,1)} async-done(((bf16[64,640]{1,0:T(8,128)(2,1)}), bf16[2048,640]{1,0:T(8,128)(2,1)}) %all-gather.2.cloned.1.call-update) | async-done | bytes 2621456 | tf_op jit(solution)/shard_map/all_gather | solution.py:39
  136.6 4.5 %copy.4 = bf16[2048,640]{0,1:T(8,128)(2,1)} copy(bf16[2048,640]{1,0:T(8,128)(2,1)} %all-gather.2.cloned.1.call-done) | data formatting | bytes 5242880 | tf_op jit(solution)/shard_map/all_gather | solution.py:39
  141.0 3.5 %reshape.28 = bf16[2048,32,20]{0,2,1:T(8,128)(2,1)S(1)} reshape(bf16[2048,640]{0,1:T(8,128)(2,1)} %copy.4) | data formatting | bytes 5242880 | tf_op jit(solution)/shard_map/reshape | solution.py:40
  144.6 1.1 slice.36
  145.6 1.4 slice_bitcast_fusion.1
  147.1 1.5 copy.5
  148.5 2.3 copy.6
  150.8 1.8 pad_bitcast_fusion.1
  152.6 1.3 copy.7
  153.9 0.5 copy.8
  154.4 3.6 %pad_maximum_fusion.1.h = bf16[2048,1024]{1,0:T(8,128)(2,1)} fusion(bf16[2048,256]{1,0:T(8,128)(2,1)S(1)} %copy.8, bf16[2048,256]{1,0:T(8,128)(2,1)} %copy.7, bf16[2048,256]{1,0:T(8,128)(2,1)} %copy.6, bf16[2048,256]{1,0:T(8,128)(2,1)S(1)} %copy.5), kind=kLoop, calls=%fused_computation.1 | loop fusion | flops 16777216 | bytes 8388608 | tf_op jit(solution)/shard_map/concatenate | solution.py:42
  158.0 118.8 %all-to-all-done = bf16[32,8,20480]{2,1,0:T(8,128)(2,1)} async-done(((bf16[32,8,20480]{2,1,0:T(8,128)(2,1)}), bf16[32,8,20480]{2,1,0:T(8,128)(2,1)}, u32[]{:S(2)}, u32[]{:S(2)}) %all-to-all-start) | async-done | bytes 10485792 | tf_op jit(solution)/shard_map/all_to_all | solution.py:53
  276.8 33.5 %shard_map.28 = bf16[2048,8192]{1,0:T(8,128)(2,1)} custom-call(bf16[2048,1024]{1,0:T(8,128)(2,1)} %pad_maximum_fusion.1.h, bf16[256,20480]{1,0:T(8,128)(2,1)} %bitcast.9.a1.a2.b, bf16[256,20480]{1,0:T(8,128)(2,1)} %bitcast.9.a1.a2.b, bf16[256,20480]{1,0:T(8,128)(2,1)} %bitcast.9.a1.a2.b), custom_call_target="tpu_custom_call" | custom-call | flops 25769803776 | bytes 33554432 | tf_op jit(solution)/shard_map/pallas_call | solution.py:30
Async XLA Ops:
  6.5 5.9 %slice-start = ((bf16[20,262144]{1,0:T(8,128)(2,1)}), bf16[4,262144]{1,0:T(4,128)(2,1)S(1)}, s32[]{:S(2)}) async-start(bf16[20,262144]{1,0:T(8,128)(2,1)} %param.3), calls=%async_computation.2 | async-start | bytes 4194304 | tf_op jit(solution)/shard_map/slice | solution.py:51
  33.9 242.8 %all-to-all-start = ((bf16[32,8,20480]{2,1,0:T(8,128)(2,1)}), bf16[32,8,20480]{2,1,0:T(8,128)(2,1)}, u32[]{:S(2)}, u32[]{:S(2)}) async-start(bf16[32,8,20480]{2,1,0:T(8,128)(2,1)} %pad_maximum_fusion), calls=%async_computation | async-start | bytes 20971520 | tf_op jit(solution)/shard_map/all_to_all | solution.py:53
  41.4 95.2 %all-gather.2.cloned.1.call-start = ((), (), s32[]{:S(2)}) async-start(), calls=%async_computation.1 | async-start | bytes 2703360 | tf_op jit(solution)/shard_map/all_gather | solution.py:39
Sparse Core Ops, SparseCore 0:
  45.1 91.4 all-gather.1

commit v2 on v0

v2 whole, which is shorter than its diff:
```python
import functools

import jax
import jax.numpy as jnp
from jax import lax
from jax.experimental import pallas as pl
from jax.experimental.pallas import tpu as pltpu
from jax.sharding import PartitionSpec as P

MESH = pl.DeviceIdType.MESH
NZ, NP = 4, 8
N = NZ * NP
ROWS, BLK, D = 2048, 64, 640
KA = 16
KB = 4
COLS = 8192
WID = 2048
NCH = COLS // WID
NPRE = NCH - 1
LOOK = 2
TN = 256
TM = 512


def send_order():
    order = []
    for m in range(NP):
        order += [(2, m), (1, m), (3, m)]
        if m:
            order.append((0, m))
    return order


ORDER = send_order()


def product(hp_ref, ra, rb, m, n):
    a = jnp.dot(hp_ref[m, 0 : N * KA], ra[:, n], preferred_element_type=jnp.float32)
    b = jnp.dot(hp_ref[m, N * KA : D], rb[:, n], preferred_element_type=jnp.float32)
    return (a + b).astype(jnp.bfloat16)


def exchange(h_ref, w_ref, y0, y1, y2, hp_ref, ra_last, rb_last, ra, rb, rbp, hraw, bsrc,
             loc, hz_s, hz_r, hp_s, hp_r, a_s, a_r, b_s, b_r):
    i, j = lax.axis_index("dp"), lax.axis_index("tp")
    me = i * NP + j

    bcopy = pltpu.make_async_copy(w_ref.at[KA : KA + KB, :], bsrc, loc.at[0])
    bcopy.start()
    hown = pltpu.make_async_copy(h_ref, hraw.at[j, i], loc.at[1])
    hown.start()

    barrier = pltpu.get_barrier_semaphore()

    def peer(kz, kp):
        return {"dp": i ^ kz, "tp": j ^ kp}

    for kz, kp in ORDER:
        pl.semaphore_signal(barrier, inc=1, device_id=peer(kz, kp), device_id_type=MESH)
    pl.semaphore_wait(barrier, N - 1)

    def dst_a(c):
        return ra.at[c] if c < NPRE else ra_last

    def dst_b(c):
        return rb.at[c] if c < NPRE else rb_last

    def cols(dev, c):
        return pl.ds(pl.multiple_of(dev * COLS + c * WID, WID), WID)

    def rows_a():
        return pl.ds(pl.multiple_of(me * KA, KA), KA)

    def send_a(c):
        for kz, kp in ORDER:
            dev = (i ^ kz) * NP + (j ^ kp)
            pltpu.make_async_remote_copy(
                w_ref.at[0:KA, cols(dev, c)], dst_a(c).at[rows_a(), :],
                a_s.at[c], a_r.at[c], device_id=peer(kz, kp), device_id_type=MESH).start()
        pltpu.make_async_copy(w_ref.at[0:KA, cols(me, c)], dst_a(c).at[rows_a(), :], a_r.at[c]).start()

    def send_b(c):
        for kz, kp in ORDER:
            dev = (i ^ kz) * NP + (j ^ kp)
            pltpu.make_async_remote_copy(
                bsrc.at[:, cols(dev, c)], dst_b(c).at[me],
                b_s.at[c], b_r.at[c], device_id=peer(kz, kp), device_id_type=MESH).start()
        pltpu.make_async_copy(w_ref.at[KA : KA + KB, cols(me, c)], dst_b(c).at[me], b_r.at[c]).start()

    for kz in (2, 3, 1):
        pltpu.make_async_remote_copy(
            h_ref, hraw.at[j, i], hz_s, hz_r, device_id=peer(kz, 0), device_id_type=MESH).start()
    send_a(0)
    bcopy.wait()
    send_b(0)
    hown.wait()
    pltpu.make_async_copy(hraw.at[j, 0:3], hraw.at[j, 0:3], hz_r).wait()
    for kp in range(1, NP):
        pltpu.make_async_remote_copy(
            hraw.at[j], hraw.at[j], hp_s, hp_r, device_id=peer(0, kp), device_id_type=MESH).start()
    for c in range(1, LOOK):
        send_a(c)
        send_b(c)

    pltpu.make_async_copy(hraw.at[0 : NP - 1], hraw.at[0 : NP - 1], hp_r).wait()
    row = lax.broadcasted_iota(jnp.int32, (D, D), 0)
    col = lax.broadcasted_iota(jnp.int32, (D, D), 1)
    src = (row * 3277) >> 16
    r = row - src * (KA + KB)
    to = jnp.where(r < KA, src * KA + r, N * KA + src * KB + r - KA)
    perm = jnp.where(to == col, 1.0, 0.0).astype(jnp.bfloat16)
    for p in range(NP):
        x = hraw[p].reshape(NZ * BLK, D)
        x = jnp.dot(x, perm, preferred_element_type=jnp.float32).astype(jnp.bfloat16)
        for z in range(NZ):
            hp_ref[pl.ds((z * NP + p) * BLK, BLK), :] = x[z * BLK : (z + 1) * BLK]

    for c in range(NCH):
        if c + LOOK < NCH:
            send_a(c + LOOK)
            send_b(c + LOOK)
        pltpu.make_async_copy(dst_a(c), dst_a(c), a_r.at[c]).wait()
        pltpu.make_async_copy(dst_b(c), dst_b(c), b_r.at[c]).wait()
        if c < NPRE:
            rbp[...] = rb[c].reshape(N * KB, WID)

            @pl.loop(0, WID // TN)
            def _(t):
                n = pl.ds(pl.multiple_of(t * TN, TN), TN)

                @pl.loop(0, ROWS // TM)
                def _(u):
                    m = pl.ds(pl.multiple_of(u * TM, TM), TM)
                    (y0, y1, y2)[c][m, n] = product(hp_ref, ra.at[c], rbp, m, n)

    pltpu.make_async_copy(hraw.at[0, 0:3], hraw.at[0, 0:3], hz_s).wait()
    pltpu.make_async_copy(hraw.at[0 : NP - 1], hraw.at[0 : NP - 1], hp_s).wait()
    for c in range(NCH):
        part = ra_last.at[0 : (N - 1) * KA, :]
        pltpu.make_async_copy(part, part, a_s.at[c]).wait()
        part = rb_last.at[0 : N - 1]
        pltpu.make_async_copy(part, part, b_s.at[c]).wait()


def finish(y0, y1, y2, hp_ref, ra, rb, out_ref, rbp, ybuf, sem_pre, sem):
    copies = []
    for t, y in enumerate((y0, y1, y2)):
        c = pltpu.make_async_copy(y, out_ref.at[:, t * WID : (t + 1) * WID], sem_pre.at[t])
        c.start()
        copies.append(c)
    rbp[...] = rb[...].reshape(N * KB, WID)
    for t in range(WID // TN):
        n = pl.ds(t * TN, TN)

        @pl.loop(0, ROWS // TM)
        def _(u):
            m = pl.ds(pl.multiple_of(u * TM, TM), TM)
            ybuf[m, n] = product(hp_ref, ra, rbp, m, n)

        c = pltpu.make_async_copy(ybuf.at[:, n], out_ref.at[:, pl.ds(NPRE * WID + t * TN, TN)], sem.at[t])
        c.start()
        copies.append(c)
    for c in copies:
        c.wait()


def local_part(h, w):
    bf = jnp.bfloat16
    any_, vmem = pl.BlockSpec(memory_space=pl.ANY), pl.BlockSpec(memory_space=pltpu.VMEM)
    dma = pltpu.SemaphoreType.DMA
    *ys, hp, ra, rb = pl.pallas_call(
        exchange,
        out_shape=(*[pltpu.VMEM((ROWS, WID), bf)] * NPRE, pltpu.VMEM((ROWS, D), bf),
                   pltpu.VMEM((N * KA, WID), bf), pltpu.VMEM((N, KB, WID), bf)),
        in_specs=[any_, any_],
        out_specs=(vmem,) * (NPRE + 3),
        scratch_shapes=[
            pltpu.VMEM((NPRE, N * KA, WID), bf), pltpu.VMEM((NPRE, N, KB, WID), bf),
            pltpu.VMEM((N * KB, WID), bf), pltpu.VMEM((NP, NZ, BLK, D), bf), pltpu.VMEM((KB, N * COLS), bf),
            dma((2,)), dma, dma, dma, dma, dma((NCH,)), dma((NCH,)), dma((NCH,)), dma((NCH,)),
        ],
        compiler_params=pltpu.CompilerParams(
            collective_id=0, has_side_effects=True, vmem_limit_bytes=20 * 2**20),
        name="exchange",
    )(h, w)
    return pl.pallas_call(
        finish,
        out_shape=jax.ShapeDtypeStruct((ROWS, COLS), bf),
        in_specs=[vmem] * (NPRE + 3),
        out_specs=any_,
        scratch_shapes=[pltpu.VMEM((N * KB, WID), bf), pltpu.VMEM((ROWS, WID), bf), dma((8,)), dma((WID // TN,))],
        compiler_params=pltpu.CompilerParams(vmem_limit_bytes=20 * 2**20),
        name="finish",
    )(*ys, hp, ra, rb)


def solution(mesh):
    return jax.shard_map(
        local_part,
        mesh=mesh,
        in_specs=(P(("dp", "tp"), None), P(("dp", "tp"), None)),
        out_specs=P(None, ("dp", "tp")),
        check_vma=False,
    )
```

time: 465 us -> 258 us (0.55)
  Pallas kernels: 0 us -> 257 us
  waiting for transfers between devices: 240 us -> 0 us
  blocking collectives: 121 us -> 0 us
  local copies, waits for them, and re-layouts: 49.7 us -> 0.89 us
  matrix products: 34.4 us -> 0 us
  between operations: 13.4 us -> 0.01 us
  starting transfers between devices: 6.21 us -> 0 us
    pallas_call x0 -> x2, Pallas kernels: none -> 257 us  [the longest x1 244 us: local_part(): pl.pallas_call(exchange, out_shape=(*[pltpu.VMEM((ROWS, WID), bf)] * NPRE...]
    all_gather x1 -> x0, waiting for transfers between devices: 199 us -> none  [local_part(): full_hidden = lax.all_gather(hid_blk, ('dp', 'tp'), axis=0, tiled=True)]
    all_to_all x1 -> x0, blocking collectives: 121 us -> none  [local_part(): w_step = lax.all_to_all(w_split, 'tp', 2, 0, tiled=True)]
    all_to_all x1 -> x0, waiting for transfers between devices: 40.5 us -> none  [local_part(): w_cols = lax.all_to_all(w_step, 'dp', 1, 0, tiled=True)]
    dot_general x1 -> x0, matrix products: 34.4 us -> none  [local_part(): jnp.dot(full_hidden, w_cols, preferred_element_type=jnp.float32)]
    reshape x2 -> x0, local copies, waits for them, and re-layouts: 21.4 us -> none  [local_part(): w_split = w_blk.reshape(rows_loc, outer_size, inner_size, col_width)]
    all_to_all x1 -> x0, local copies, waits for them, and re-layouts: 13.8 us -> none  [local_part(): w_step = lax.all_to_all(w_split, 'tp', 2, 0, tiled=True)]
    unnamed x1 -> x2, local copies, waits for them, and re-layouts: 14.4 us -> 0.89 us
  transfers between devices with their start and end apart: 2 -> 0, of which waited for: 2 -> 0; matrix products, arithmetic and copies ran while one was open for 0% -> 0% of each run, Pallas kernels for 0% -> 0%
where the time goes in v2:
time: 258 us
  Pallas kernels  257 us (100%)
    pallas_call x1, Pallas kernels, local_part(): pl.pallas_call(exchange, out_shape=(*[pltpu.VMEM((ROWS, WID), bf)] * NPRE...  244 us
    pallas_call x1, Pallas kernels, local_part(): pl.pallas_call(finish, out_shape=jax.ShapeDtypeStruct((ROWS, COLS), bf),...  12.6 us

profile of v2, /device:TPU:0, one launch (start us, length us, event | category | flops | bytes accessed | tf_op | source)
XLA Modules:
  0.0 257.9 jit_solution(1784585468139038448)
XLA Ops:
  0.0 0.0 copy-start
  0.0 0.9 copy-done
  0.9 244.3 %exchange.1 = (bf16[2048,2048]{1,0:T(8,128)(2,1)S(1)}, bf16[2048,2048]{1,0:T(8,128)(2,1)S(1)}, bf16[2048,2048]{1,0:T(8,128)(2,1)S(1)}, bf16[2048,640]{1,0:T(8,12...) custom-call(bf16[64,640]{1,0:T(8,128)(2,1)S(1)} %copy-done, bf16[20,262144]{1,0:T(8,128)(2,1)} %w_ref.1), custom_call_target="tpu_custom_call" | custom-call | tf_op jit(solution)/shard_map/exchange/pallas_call | solution.py:171
  245.2 12.6 %finish.1 = bf16[2048,8192]{1,0:T(8,128)(2,1)} custom-call(bf16[2048,2048]{1,0:T(8,128)(2,1)S(1)} %get-tuple-element.11.y0, bf16[2048,2048]{1,0:T(8,128)(2,1)S(1)} %get-tuple-element.12.y1, bf16[2048,2048]{1,0:T(8,128)(2,1)S(1)} %get-tuple-element.13.y2, bf16[2048,640]{1,0:T(8,128)(2,1)S(1)} %get-tuple-element.14.hp_ref, ...), custom_call_target="tpu_custom_call" | custom-call | tf_op jit(solution)/shard_map/finish/pallas_call | solution.py:186
Async XLA Ops:
  0.0 0.9 copy-start

commit v3 on v2

v3 whole, which is shorter than its diff:
```python
import jax
import jax.numpy as jnp
from jax import lax
from jax.experimental import pallas as pl
from jax.experimental.pallas import tpu as pltpu
from jax.sharding import PartitionSpec as P

MESH = pl.DeviceIdType.MESH
NZ, NP = 4, 8
N = NZ * NP
ROWS, BLK, D = 2048, 64, 640
KA = 16
KB = 4
COLS = 8192
WIDS = (2560, 2560, 2048, 1024)
OFFS = tuple(sum(WIDS[:c]) for c in range(len(WIDS)))
NCH = len(WIDS)
NPRE = NCH - 1
LOOK = 3
TN = 256
TM = 512

MSEQ = (0, 2, 4, 3, 1, 6, 5, 7)
CROSS = [(kz, m) for m in MSEQ for kz in (2, 3)]
STAY = [(kz, m) for m in MSEQ for kz in (1, 0) if (kz, m) != (0, 0)]


def product(hp_ref, ra, rb, m, n):
    a = jnp.dot(hp_ref[m, 0 : N * KA], ra[:, n], preferred_element_type=jnp.float32)
    b = jnp.dot(hp_ref[m, N * KA : D], rb[:, n], preferred_element_type=jnp.float32)
    return (a + b).astype(jnp.bfloat16)


def exchange(h_ref, w_ref, *refs):
    ys, (hp_ref, ra_last, rb_last), refs = refs[:NPRE], refs[NPRE : NPRE + 3], refs[NPRE + 3 :]
    ras, rbs, rbps, refs = refs[:NPRE], refs[NPRE : 2 * NPRE], refs[2 * NPRE : 3 * NPRE], refs[3 * NPRE :]
    hraw, bsrc, loc, hz_s, hm_r, hn_r, hp_s, hp_r, a_s, a_r, b_s, b_r = refs
    ras, rbs = (*ras, ra_last), (*rbs, rb_last)
    i, j = lax.axis_index("dp"), lax.axis_index("tp")
    me = i * NP + j
    inner = jnp.logical_and(i >= 1, i <= 2)

    bcopy = pltpu.make_async_copy(w_ref.at[KA : KA + KB, :], bsrc, loc.at[0])
    bcopy.start()
    hown = pltpu.make_async_copy(h_ref, hraw.at[j, i], loc.at[1])
    hown.start()

    barrier = pltpu.get_barrier_semaphore()

    def peer(kz, kp):
        return {"dp": i ^ kz, "tp": j ^ kp}

    for kz, kp in CROSS + STAY:
        pl.semaphore_signal(barrier, inc=1, device_id=peer(kz, kp), device_id_type=MESH)
    pl.semaphore_wait(barrier, N - 1)

    def remote(src, dst, s, r, to):
        return pltpu.make_async_remote_copy(src, dst, s, r, device_id=to, device_id_type=MESH)

    def cols(dev, c):
        return pl.ds(pl.multiple_of(dev * COLS + OFFS[c], 256), WIDS[c])

    rows_a = pl.ds(pl.multiple_of(me * KA, KA), KA)

    def send_list(c, order):
        for kz, kp in order:
            dev = (i ^ kz) * NP + (j ^ kp)
            remote(w_ref.at[0:KA, cols(dev, c)], ras[c].at[rows_a, :], a_s.at[c], a_r.at[c], peer(kz, kp)).start()
            remote(bsrc.at[:, cols(dev, c)], rbs[c].at[me], b_s.at[c], b_r.at[c], peer(kz, kp)).start()

    def send(c):
        @pl.when(inner)
        def _():
            send_list(c, CROSS + STAY)

        @pl.when(jnp.logical_not(inner))
        def _():
            send_list(c, STAY + CROSS)

        pltpu.make_async_copy(w_ref.at[0:KA, cols(me, c)], ras[c].at[rows_a, :], a_r.at[c]).start()
        pltpu.make_async_copy(w_ref.at[KA : KA + KB, cols(me, c)], rbs[c].at[me], b_r.at[c]).start()

    mirror = {"dp": NZ - 1 - i, "tp": j}
    remote(h_ref, hraw.at[j, i], hz_s, hm_r, mirror).start()
    remote(h_ref, hraw.at[j, i], hz_s, hn_r, peer(1, 0)).start()
    bcopy.wait()
    send(0)
    got = hraw.at[j, NZ - 1 - i]
    pltpu.make_async_copy(got, got, hm_r).wait()
    remote(got, got, hz_s, hn_r, peer(1, 0)).start()
    hown.wait()
    pltpu.make_async_copy(hraw.at[j, 0:2], hraw.at[j, 0:2], hn_r).wait()
    for kp in range(1, NP):
        remote(hraw.at[j], hraw.at[j], hp_s, hp_r, peer(0, kp)).start()
    for c in range(1, LOOK):
        send(c)

    pltpu.make_async_copy(hraw.at[0 : NP - 1], hraw.at[0 : NP - 1], hp_r).wait()
    row = lax.broadcasted_iota(jnp.int32, (D, D), 0)
    col = lax.broadcasted_iota(jnp.int32, (D, D), 1)
    src = (row * 3277) >> 16
    r = row - src * (KA + KB)
    to = jnp.where(r < KA, src * KA + r, N * KA + src * KB + r - KA)
    perm = jnp.where(to == col, 1.0, 0.0).astype(jnp.bfloat16)
    for p in range(NP):
        x = hraw[p].reshape(NZ * BLK, D)
        x = jnp.dot(x, perm, preferred_element_type=jnp.float32).astype(jnp.bfloat16)
        for z in range(NZ):
            hp_ref[pl.ds((z * NP + p) * BLK, BLK), :] = x[z * BLK : (z + 1) * BLK]

    for c in range(NCH):
        pltpu.make_async_copy(ras[c], ras[c], a_r.at[c]).wait()
        pltpu.make_async_copy(rbs[c], rbs[c], b_r.at[c]).wait()
        if c + LOOK < NCH:
            send(c + LOOK)
        if c < NPRE:
            rbps[c][...] = rbs[c][...].reshape(N * KB, WIDS[c])

            @pl.loop(0, WIDS[c] // TN)
            def _(t):
                n = pl.ds(pl.multiple_of(t * TN, TN), TN)

                @pl.loop(0, ROWS // TM)
                def _(u):
                    m = pl.ds(pl.multiple_of(u * TM, TM), TM)
                    ys[c][m, n] = product(hp_ref, ras[c], rbps[c], m, n)

    pltpu.make_async_copy(hraw.at[0, 0:3], hraw.at[0, 0:3], hz_s).wait()
    pltpu.make_async_copy(hraw.at[0 : NP - 1], hraw.at[0 : NP - 1], hp_s).wait()
    for c in range(NCH):
        part = ras[c].at[0 : (N - 1) * KA, :]
        pltpu.make_async_copy(part, part, a_s.at[c]).wait()
        part = rbs[c].at[0 : N - 1]
        pltpu.make_async_copy(part, part, b_s.at[c]).wait()


def finish(*refs):
    ys, (hp_ref, ra, rb, out_ref, rbp, ybuf, sem_pre, sem) = refs[:NPRE], refs[NPRE:]
    copies = []
    for c, y in enumerate(ys):
        copy = pltpu.make_async_copy(y, out_ref.at[:, OFFS[c] : OFFS[c] + WIDS[c]], sem_pre.at[c])
        copy.start()
        copies.append(copy)
    rbp[...] = rb[...].reshape(N * KB, WIDS[-1])
    for t in range(WIDS[-1] // TN):
        n = pl.ds(t * TN, TN)

        @pl.loop(0, ROWS // TM)
        def _(u):
            m = pl.ds(pl.multiple_of(u * TM, TM), TM)
            ybuf[m, n] = product(hp_ref, ra, rbp, m, n)

        copy = pltpu.make_async_copy(ybuf.at[:, n], out_ref.at[:, pl.ds(OFFS[-1] + t * TN, TN)], sem.at[t])
        copy.start()
        copies.append(copy)
    for copy in copies:
        copy.wait()


def local_part(h, w):
    bf = jnp.bfloat16
    any_, vmem = pl.BlockSpec(memory_space=pl.ANY), pl.BlockSpec(memory_space=pltpu.VMEM)
    hbm = pl.BlockSpec(memory_space=pltpu.HBM)
    dma = pltpu.SemaphoreType.DMA
    last = WIDS[-1]
    passed = pl.pallas_call(
        exchange,
        out_shape=(*[pltpu.VMEM((ROWS, wid), bf) for wid in WIDS[:NPRE]], pltpu.VMEM((ROWS, D), bf),
                   pltpu.VMEM((N * KA, last), bf), pltpu.VMEM((N, KB, last), bf)),
        in_specs=[hbm, hbm],
        out_specs=(vmem,) * (NPRE + 3),
        scratch_shapes=[
            *[pltpu.VMEM((N * KA, wid), bf) for wid in WIDS[:NPRE]],
            *[pltpu.VMEM((N, KB, wid), bf) for wid in WIDS[:NPRE]],
            *[pltpu.VMEM((N * KB, wid), bf) for wid in WIDS[:NPRE]],
            pltpu.VMEM((NP, NZ, BLK, D), bf), pltpu.VMEM((KB, N * COLS), bf),
            dma((2,)), dma, dma, dma, dma, dma, dma((NCH,)), dma((NCH,)), dma((NCH,)), dma((NCH,)),
        ],
        compiler_params=pltpu.CompilerParams(
            collective_id=0, has_side_effects=True, vmem_limit_bytes=22 * 2**20),
        name="exchange",
    )(pltpu.with_memory_space_constraint(h, pltpu.HBM), w)
    return pl.pallas_call(
        finish,
        out_shape=jax.ShapeDtypeStruct((ROWS, COLS), bf),
        in_specs=[vmem] * (NPRE + 3),
        out_specs=any_,
        scratch_shapes=[pltpu.VMEM((N * KB, last), bf), pltpu.VMEM((ROWS, last), bf), dma((NPRE,)), dma((last // TN,))],
        compiler_params=pltpu.CompilerParams(vmem_limit_bytes=22 * 2**20),
        name="finish",
    )(*passed)


def solution(mesh):
    return jax.shard_map(
        local_part,
        mesh=mesh,
        in_specs=(P(("dp", "tp"), None), P(("dp", "tp"), None)),
        out_specs=P(None, ("dp", "tp")),
        check_vma=False,
    )
```

time: 258 us -> 252 us (0.977)
  Pallas kernels: 257 us -> 251 us
    pallas_call x1, Pallas kernels: 244 us -> 240 us  [local_part(): pl.pallas_call(exchange, out_shape=(*[pltpu.VMEM((ROWS, wid), bf) for wid...]
where the time goes in v3:
time: 252 us; the launch traced here: 251 us
  Pallas kernels  251 us (100%)
    pallas_call x1, Pallas kernels, local_part(): pl.pallas_call(exchange, out_shape=(*[pltpu.VMEM((ROWS, wid), bf) for wid...  240 us
    pallas_call x1, Pallas kernels, local_part(): pl.pallas_call(finish, out_shape=jax.ShapeDtypeStruct((ROWS, COLS), bf),...  11.1 us

profile of v3, /device:TPU:0, one launch (start us, length us, event | category | flops | bytes accessed | tf_op | source)
XLA Modules:
  0.0 250.8 jit_solution(16793740471496658518)
XLA Ops:
  0.0 239.7 %exchange.1 = (bf16[2048,2560]{1,0:T(8,128)(2,1)S(1)}, bf16[2048,2560]{1,0:T(8,128)(2,1)S(1)}, bf16[2048,2048]{1,0:T(8,128)(2,1)S(1)}, bf16[2048,640]{1,0:T(8,12...) custom-call(bf16[64,640]{1,0:T(8,128)(2,1)} %h_ref.1, bf16[20,262144]{1,0:T(8,128)(2,1)} %w_ref.1), custom_call_target="tpu_custom_call" | custom-call | tf_op jit(solution)/shard_map/exchange/pallas_call | solution.py:166
  239.7 11.1 %finish.1 = bf16[2048,8192]{1,0:T(8,128)(2,1)} custom-call(bf16[2048,2560]{1,0:T(8,128)(2,1)S(1)} %get-tuple-element.11.refs_0_, bf16[2048,2560]{1,0:T(8,128)(2,1)S(1)} %get-tuple-element.12.refs_1_, bf16[2048,2048]{1,0:T(8,128)(2,1)S(1)} %get-tuple-element.13.refs_2_, bf16[2048,640]{1,0:T(8,128)(2,1)S(1)} %get-tuple-element.14.refs_3_, ...), custom_call_target="tpu_custom_call" | custom-call | tf_op jit(solution)/shard_map/finish/pallas_call | solution.py:183

commit v4 on v3

--- a/solution.py
+++ b/solution.py
@@ -25,6 +25,10 @@
 STAY = [(kz, m) for m in MSEQ for kz in (1, 0) if (kz, m) != (0, 0)]
 
 
+def plane(kz):
+    return [(kz, m) for m in MSEQ if (kz, m) != (0, 0)]
+
+
 def product(hp_ref, ra, rb, m, n):
     a = jnp.dot(hp_ref[m, 0 : N * KA], ra[:, n], preferred_element_type=jnp.float32)
     b = jnp.dot(hp_ref[m, N * KA : D], rb[:, n], preferred_element_type=jnp.float32)
@@ -34,7 +38,7 @@
 def exchange(h_ref, w_ref, *refs):
     ys, (hp_ref, ra_last, rb_last), refs = refs[:NPRE], refs[NPRE : NPRE + 3], refs[NPRE + 3 :]
     ras, rbs, rbps, refs = refs[:NPRE], refs[NPRE : 2 * NPRE], refs[2 * NPRE : 3 * NPRE], refs[3 * NPRE :]
-    hraw, bsrc, loc, hz_s, hm_r, hn_r, hp_s, hp_r, a_s, a_r, b_s, b_r = refs
+    hraw, bsrc, news, loc, hz_s, hm_r, hn_r, hp_s, hp_r, a_s, a_r, b_s, b_r = refs
     ras, rbs = (*ras, ra_last), (*rbs, rb_last)
     i, j = lax.axis_index("dp"), lax.axis_index("tp")
     me = i * NP + j
@@ -50,9 +54,18 @@
     def peer(kz, kp):
         return {"dp": i ^ kz, "tp": j ^ kp}
 
-    for kz, kp in CROSS + STAY:
-        pl.semaphore_signal(barrier, inc=1, device_id=peer(kz, kp), device_id_type=MESH)
-    pl.semaphore_wait(barrier, N - 1)
+    def tell(sem, kz, kp=0):
+        pl.semaphore_signal(sem, inc=1, device_id=peer(kz, kp), device_id_type=MESH)
+
+    for kz, kp in plane(0):
+        tell(barrier, kz, kp)
+
+    @pl.when(inner)
+    def _():
+        tell(barrier, 3)
+        tell(barrier, 1)
+
+    pl.semaphore_wait(barrier, NP)
 
     def remote(src, dst, s, r, to):
         return pltpu.make_async_remote_copy(src, dst, s, r, device_id=to, device_id_type=MESH)
@@ -77,14 +90,41 @@
         def _():
             send_list(c, STAY + CROSS)
 
+        own(c)
+
+    def own(c):
         pltpu.make_async_copy(w_ref.at[0:KA, cols(me, c)], ras[c].at[rows_a, :], a_r.at[c]).start()
         pltpu.make_async_copy(w_ref.at[KA : KA + KB, cols(me, c)], rbs[c].at[me], b_r.at[c]).start()
 
-    mirror = {"dp": NZ - 1 - i, "tp": j}
-    remote(h_ref, hraw.at[j, i], hz_s, hm_r, mirror).start()
-    remote(h_ref, hraw.at[j, i], hz_s, hn_r, peer(1, 0)).start()
-    bcopy.wait()
-    send(0)
+    def hidden(kz, r):
+        remote(h_ref, hraw.at[j, i], hz_s, r, peer(kz, 0)).start()
+
+    @pl.when(inner)
+    def _():
+        tell(news.at[0], 3)
+        hidden(3, hm_r)
+        bcopy.wait()
+        send_list(0, [(3, 0)])
+        pl.semaphore_wait(news.at[0], 1)
+        send_list(0, plane(3)[1:])
+        pl.semaphore_wait(news.at[1], 1)
+        tell(news.at[2], 3)
+        hidden(1, hn_r)
+        pl.semaphore_wait(news.at[2], 1)
+        tell(news.at[3], 1)
+        send_list(0, plane(2) + STAY)
+
+    @pl.when(jnp.logical_not(inner))
+    def _():
+        tell(news.at[1], 1)
+        hidden(1, hn_r)
+        bcopy.wait()
+        send_list(0, plane(0))
+        pl.semaphore_wait(news.at[3], 1)
+        hidden(3, hm_r)
+        send_list(0, plane(1) + CROSS)
+
+    own(0)
     got = hraw.at[j, NZ - 1 - i]
     pltpu.make_async_copy(got, got, hm_r).wait()
     remote(got, got, hz_s, hn_r, peer(1, 0)).start()
@@ -137,22 +177,26 @@
 def finish(*refs):
     ys, (hp_ref, ra, rb, out_ref, rbp, ybuf, sem_pre, sem) = refs[:NPRE], refs[NPRE:]
     copies = []
-    for c, y in enumerate(ys):
-        copy = pltpu.make_async_copy(y, out_ref.at[:, OFFS[c] : OFFS[c] + WIDS[c]], sem_pre.at[c])
-        copy.start()
+
+    def put(src, u, c, s):
+        m = pl.ds(u * TM, TM)
+        copy = pltpu.make_async_copy(src.at[m, :], out_ref.at[m, OFFS[c] : OFFS[c] + WIDS[c]], s)
+        copy.start(priority=len(copies) % 2)
         copies.append(copy)
+
+    for u in range(ROWS // TM):
+        for c, y in enumerate(ys):
+            put(y, u, c, sem_pre.at[c, u])
     rbp[...] = rb[...].reshape(N * KB, WIDS[-1])
-    for t in range(WIDS[-1] // TN):
-        n = pl.ds(t * TN, TN)
-
-        @pl.loop(0, ROWS // TM)
-        def _(u):
-            m = pl.ds(pl.multiple_of(u * TM, TM), TM)
+    for u in range(ROWS // TM):
+        m = pl.ds(u * TM, TM)
+
+        @pl.loop(0, WIDS[-1] // TN)
+        def _(t):
+            n = pl.ds(pl.multiple_of(t * TN, TN), TN)
             ybuf[m, n] = product(hp_ref, ra, rbp, m, n)
 
-        copy = pltpu.make_async_copy(ybuf.at[:, n], out_ref.at[:, pl.ds(OFFS[-1] + t * TN, TN)], sem.at[t])
-        copy.start()
-        copies.append(copy)
+        put(ybuf, u, NCH - 1, sem.at[u])
     for copy in copies:
         copy.wait()
 
@@ -174,7 +218,7 @@
             *[pltpu.VMEM((N, KB, wid), bf) for wid in WIDS[:NPRE]],
             *[pltpu.VMEM((N * KB, wid), bf) for wid in WIDS[:NPRE]],
             pltpu.VMEM((NP, NZ, BLK, D), bf), pltpu.VMEM((KB, N * COLS), bf),
-            dma((2,)), dma, dma, dma, dma, dma, dma((NCH,)), dma((NCH,)), dma((NCH,)), dma((NCH,)),
+            pltpu.SemaphoreType.REGULAR((4,)), dma((2,)), dma, dma, dma, dma, dma, dma((NCH,)), dma((NCH,)), dma((NCH,)), dma((NCH,)),
         ],
         compiler_params=pltpu.CompilerParams(
             collective_id=0, has_side_effects=True, vmem_limit_bytes=22 * 2**20),
@@ -185,7 +229,7 @@
         out_shape=jax.ShapeDtypeStruct((ROWS, COLS), bf),
         in_specs=[vmem] * (NPRE + 3),
         out_specs=any_,
-        scratch_shapes=[pltpu.VMEM((N * KB, last), bf), pltpu.VMEM((ROWS, last), bf), dma((NPRE,)), dma((last // TN,))],
+        scratch_shapes=[pltpu.VMEM((N * KB, last), bf), pltpu.VMEM((ROWS, last), bf), dma((NPRE, ROWS // TM)), dma((ROWS // TM,))],
         compiler_params=pltpu.CompilerParams(vmem_limit_bytes=22 * 2**20),
         name="finish",
     )(*passed)

time: 252 us -> 250 us (level)
  no operation moved by 1% of the time
where the time goes in v4:
time: 250 us; the launch traced here: 249 us
  Pallas kernels  249 us (100%)
    pallas_call x1, Pallas kernels, local_part(): pl.pallas_call(exchange, out_shape=(*[pltpu.VMEM((ROWS, wid), bf) for wid...  238 us
    pallas_call x1, Pallas kernels, local_part(): pl.pallas_call(finish, out_shape=jax.ShapeDtypeStruct((ROWS, COLS), bf),...  11 us

profile of v4, /device:TPU:0, one launch (start us, length us, event | category | flops | bytes accessed | tf_op | source)
XLA Modules:
  0.0 248.6 jit_solution(14511493713840949705)
XLA Ops:
  0.0 237.6 %exchange.1 = (bf16[2048,2560]{1,0:T(8,128)(2,1)S(1)}, bf16[2048,2560]{1,0:T(8,128)(2,1)S(1)}, bf16[2048,2048]{1,0:T(8,128)(2,1)S(1)}, bf16[2048,640]{1,0:T(8,12...) custom-call(bf16[64,640]{1,0:T(8,128)(2,1)} %h_ref.1, bf16[20,262144]{1,0:T(8,128)(2,1)} %w_ref.1), custom_call_target="tpu_custom_call" | custom-call | tf_op jit(solution)/shard_map/exchange/pallas_call | solution.py:210
  237.6 11.0 %finish.1 = bf16[2048,8192]{1,0:T(8,128)(2,1)} custom-call(bf16[2048,2560]{1,0:T(8,128)(2,1)S(1)} %get-tuple-element.11.refs_0_, bf16[2048,2560]{1,0:T(8,128)(2,1)S(1)} %get-tuple-element.12.refs_1_, bf16[2048,2048]{1,0:T(8,128)(2,1)S(1)} %get-tuple-element.13.refs_2_, bf16[2048,640]{1,0:T(8,128)(2,1)S(1)} %get-tuple-element.14.refs_3_, ...), custom_call_target="tpu_custom_call" | custom-call | tf_op jit(solution)/shard_map/finish/pallas_call | solution.py:227

commit v5 on v4

--- a/solution.py
+++ b/solution.py
@@ -65,6 +65,7 @@
         tell(barrier, 3)
         tell(barrier, 1)
 
+    hown.wait()
     pl.semaphore_wait(barrier, NP)
 
     def remote(src, dst, s, r, to):
@@ -82,13 +83,16 @@
             remote(bsrc.at[:, cols(dev, c)], rbs[c].at[me], b_s.at[c], b_r.at[c], peer(kz, kp)).start()
 
     def send(c):
-        @pl.when(inner)
-        def _():
-            send_list(c, CROSS + STAY)
-
-        @pl.when(jnp.logical_not(inner))
-        def _():
+        if c >= 2:
             send_list(c, STAY + CROSS)
+        else:
+            @pl.when(inner)
+            def _():
+                send_list(c, CROSS + STAY)
+
+            @pl.when(jnp.logical_not(inner))
+            def _():
+                send_list(c, STAY + CROSS)
 
         own(c)
 
@@ -97,7 +101,7 @@
         pltpu.make_async_copy(w_ref.at[KA : KA + KB, cols(me, c)], rbs[c].at[me], b_r.at[c]).start()
 
     def hidden(kz, r):
-        remote(h_ref, hraw.at[j, i], hz_s, r, peer(kz, 0)).start()
+        remote(hraw.at[j, i], hraw.at[j, i], hz_s, r, peer(kz, 0)).start()
 
     @pl.when(inner)
     def _():
@@ -128,7 +132,6 @@
     got = hraw.at[j, NZ - 1 - i]
     pltpu.make_async_copy(got, got, hm_r).wait()
     remote(got, got, hz_s, hn_r, peer(1, 0)).start()
-    hown.wait()
     pltpu.make_async_copy(hraw.at[j, 0:2], hraw.at[j, 0:2], hn_r).wait()
     for kp in range(1, NP):
         remote(hraw.at[j], hraw.at[j], hp_s, hp_r, peer(0, kp)).start()

time: 250 us -> 251 us (level)
  no operation moved by 1% of the time
where the time goes in v5:
time: 251 us; the launch traced here: 249 us
  Pallas kernels  249 us (99%)
    pallas_call x1, Pallas kernels, local_part(): pl.pallas_call(exchange, out_shape=(*[pltpu.VMEM((ROWS, wid), bf) for wid...  238 us
    pallas_call x1, Pallas kernels, local_part(): pl.pallas_call(finish, out_shape=jax.ShapeDtypeStruct((ROWS, COLS), bf),...  11 us

profile of v5, /device:TPU:0, one launch (start us, length us, event | category | flops | bytes accessed | tf_op | source)
XLA Modules:
  0.0 249.2 jit_solution(12280377364518139033)
XLA Ops:
  0.0 238.2 %exchange.1 = (bf16[2048,2560]{1,0:T(8,128)(2,1)S(1)}, bf16[2048,2560]{1,0:T(8,128)(2,1)S(1)}, bf16[2048,2048]{1,0:T(8,128)(2,1)S(1)}, bf16[2048,640]{1,0:T(8,12...) custom-call(bf16[64,640]{1,0:T(8,128)(2,1)} %h_ref.1, bf16[20,262144]{1,0:T(8,128)(2,1)} %w_ref.1), custom_call_target="tpu_custom_call" | custom-call | tf_op jit(solution)/shard_map/exchange/pallas_call | solution.py:213
  238.2 11.0 %finish.1 = bf16[2048,8192]{1,0:T(8,128)(2,1)} custom-call(bf16[2048,2560]{1,0:T(8,128)(2,1)S(1)} %get-tuple-element.11.refs_0_, bf16[2048,2560]{1,0:T(8,128)(2,1)S(1)} %get-tuple-element.12.refs_1_, bf16[2048,2048]{1,0:T(8,128)(2,1)S(1)} %get-tuple-element.13.refs_2_, bf16[2048,640]{1,0:T(8,128)(2,1)S(1)} %get-tuple-element.14.refs_3_, ...), custom_call_target="tpu_custom_call" | custom-call | tf_op jit(solution)/shard_map/finish/pallas_call | solution.py:230

commit v6 on v4

--- a/solution.py
+++ b/solution.py
@@ -57,15 +57,17 @@
     def tell(sem, kz, kp=0):
         pl.semaphore_signal(sem, inc=1, device_id=peer(kz, kp), device_id_type=MESH)
 
-    for kz, kp in plane(0):
-        tell(barrier, kz, kp)
-
     @pl.when(inner)
     def _():
         tell(barrier, 3)
         tell(barrier, 1)
-
-    pl.semaphore_wait(barrier, NP)
+        pl.semaphore_wait(barrier, 1)
+
+    @pl.when(jnp.logical_not(inner))
+    def _():
+        for kz, kp in plane(0):
+            tell(barrier, kz, kp)
+        pl.semaphore_wait(barrier, NP)
 
     def remote(src, dst, s, r, to):
         return pltpu.make_async_remote_copy(src, dst, s, r, device_id=to, device_id_type=MESH)
@@ -75,16 +77,23 @@
 
     rows_a = pl.ds(pl.multiple_of(me * KA, KA), KA)
 
+    def send_a(c, kz, kp):
+        dev = (i ^ kz) * NP + (j ^ kp)
+        remote(w_ref.at[0:KA, cols(dev, c)], ras[c].at[rows_a, :], a_s.at[c], a_r.at[c], peer(kz, kp)).start()
+
+    def send_b(c, kz, kp):
+        dev = (i ^ kz) * NP + (j ^ kp)
+        remote(bsrc.at[:, cols(dev, c)], rbs[c].at[me], b_s.at[c], b_r.at[c], peer(kz, kp)).start()
+
     def send_list(c, order):
         for kz, kp in order:
-            dev = (i ^ kz) * NP + (j ^ kp)
-            remote(w_ref.at[0:KA, cols(dev, c)], ras[c].at[rows_a, :], a_s.at[c], a_r.at[c], peer(kz, kp)).start()
-            remote(bsrc.at[:, cols(dev, c)], rbs[c].at[me], b_s.at[c], b_r.at[c], peer(kz, kp)).start()
+            send_a(c, kz, kp)
+            send_b(c, kz, kp)
 
     def send(c):
         @pl.when(inner)
         def _():
-            send_list(c, CROSS + STAY)
+            send_list(c, [k for k in CROSS if c >= LOOK or k != (3, 0)] + STAY)
 
         @pl.when(jnp.logical_not(inner))
         def _():
@@ -101,28 +110,32 @@
 
     @pl.when(inner)
     def _():
-        tell(news.at[0], 3)
         hidden(3, hm_r)
+        for c in range(LOOK):
+            send_a(c, 3, 0)
         bcopy.wait()
-        send_list(0, [(3, 0)])
-        pl.semaphore_wait(news.at[0], 1)
-        send_list(0, plane(3)[1:])
+        for c in range(LOOK):
+            send_b(c, 3, 0)
         pl.semaphore_wait(news.at[1], 1)
         tell(news.at[2], 3)
         hidden(1, hn_r)
         pl.semaphore_wait(news.at[2], 1)
         tell(news.at[3], 1)
-        send_list(0, plane(2) + STAY)
+        send_list(0, plane(3)[1:] + plane(2) + STAY)
 
     @pl.when(jnp.logical_not(inner))
     def _():
-        tell(news.at[1], 1)
+        for kz, kp in plane(0):
+            tell(news.at[0], kz, kp)
         hidden(1, hn_r)
         bcopy.wait()
         send_list(0, plane(0))
+        pl.semaphore_wait(news.at[0], NP - 1)
+        tell(news.at[1], 1)
+        send_list(0, plane(1))
         pl.semaphore_wait(news.at[3], 1)
         hidden(3, hm_r)
-        send_list(0, plane(1) + CROSS)
+        send_list(0, CROSS)
 
     own(0)
     got = hraw.at[j, NZ - 1 - i]

time: 250 us -> 248 us (level)
  Pallas kernels: 249 us -> 246 us
where the time goes in v6:
time: 248 us; the launch traced here: 246 us
  Pallas kernels  246 us (99%)
    pallas_call x1, Pallas kernels, local_part(): pl.pallas_call(exchange, out_shape=(*[pltpu.VMEM((ROWS, wid), bf) for wid...  235 us
    pallas_call x1, Pallas kernels, local_part(): pl.pallas_call(finish, out_shape=jax.ShapeDtypeStruct((ROWS, COLS), bf),...  11 us

profile of v6, /device:TPU:0, one launch (start us, length us, event | category | flops | bytes accessed | tf_op | source)
XLA Modules:
  0.0 246.2 jit_solution(8643057168948570836)
XLA Ops:
  0.0 235.2 %exchange.1 = (bf16[2048,2560]{1,0:T(8,128)(2,1)S(1)}, bf16[2048,2560]{1,0:T(8,128)(2,1)S(1)}, bf16[2048,2048]{1,0:T(8,128)(2,1)S(1)}, bf16[2048,640]{1,0:T(8,12...) custom-call(bf16[64,640]{1,0:T(8,128)(2,1)} %h_ref.1, bf16[20,262144]{1,0:T(8,128)(2,1)} %w_ref.1), custom_call_target="tpu_custom_call" | custom-call | tf_op jit(solution)/shard_map/exchange/pallas_call | solution.py:223
  235.2 11.0 %finish.1 = bf16[2048,8192]{1,0:T(8,128)(2,1)} custom-call(bf16[2048,2560]{1,0:T(8,128)(2,1)S(1)} %get-tuple-element.11.refs_0_, bf16[2048,2560]{1,0:T(8,128)(2,1)S(1)} %get-tuple-element.12.refs_1_, bf16[2048,2048]{1,0:T(8,128)(2,1)S(1)} %get-tuple-element.13.refs_2_, bf16[2048,640]{1,0:T(8,128)(2,1)S(1)} %get-tuple-element.14.refs_3_, ...), custom_call_target="tpu_custom_call" | custom-call | tf_op jit(solution)/shard_map/finish/pallas_call | solution.py:240

commit v7 on v6

--- a/solution.py
+++ b/solution.py
@@ -12,10 +12,11 @@
 KA = 16
 KB = 4
 COLS = 8192
-WIDS = (2560, 2560, 2048, 1024)
+WIDS = (2304, 2048, 1536, 1024, 512, 512, 256)
 OFFS = tuple(sum(WIDS[:c]) for c in range(len(WIDS)))
 NCH = len(WIDS)
-NPRE = NCH - 1
+NPRE = 5
+NLATE = NCH - NPRE
 LOOK = 3
 TN = 256
 TM = 512
@@ -36,10 +37,11 @@
 
 
 def exchange(h_ref, w_ref, *refs):
-    ys, (hp_ref, ra_last, rb_last), refs = refs[:NPRE], refs[NPRE : NPRE + 3], refs[NPRE + 3 :]
+    ys, hp_ref, refs = refs[:NPRE], refs[NPRE], refs[NPRE + 1 :]
+    late, refs = refs[: 2 * NLATE], refs[2 * NLATE :]
     ras, rbs, rbps, refs = refs[:NPRE], refs[NPRE : 2 * NPRE], refs[2 * NPRE : 3 * NPRE], refs[3 * NPRE :]
     hraw, bsrc, news, loc, hz_s, hm_r, hn_r, hp_s, hp_r, a_s, a_r, b_s, b_r = refs
-    ras, rbs = (*ras, ra_last), (*rbs, rb_last)
+    ras, rbs = (*ras, *late[:NLATE]), (*rbs, *late[NLATE:])
     i, j = lax.axis_index("dp"), lax.axis_index("tp")
     me = i * NP + j
     inner = jnp.logical_and(i >= 1, i <= 2)
@@ -188,28 +190,30 @@
 
 
 def finish(*refs):
-    ys, (hp_ref, ra, rb, out_ref, rbp, ybuf, sem_pre, sem) = refs[:NPRE], refs[NPRE:]
+    ys, hp_ref, refs = refs[:NPRE], refs[NPRE], refs[NPRE + 1 :]
+    ras, rbs, out_ref, refs = refs[:NLATE], refs[NLATE : 2 * NLATE], refs[2 * NLATE], refs[2 * NLATE + 1 :]
+    rbps, (ybuf, sem_pre, sem) = refs[:NLATE], refs[NLATE:]
     copies = []
 
-    def put(src, u, c, s):
+    def put(src, u, off, wid, s):
         m = pl.ds(u * TM, TM)
-        copy = pltpu.make_async_copy(src.at[m, :], out_ref.at[m, OFFS[c] : OFFS[c] + WIDS[c]], s)
+        copy = pltpu.make_async_copy(src.at[m, :], out_ref.at[m, off : off + wid], s)
         copy.start(priority=len(copies) % 2)
         copies.append(copy)
 
     for u in range(ROWS // TM):
         for c, y in enumerate(ys):
-            put(y, u, c, sem_pre.at[c, u])
-    rbp[...] = rb[...].reshape(N * KB, WIDS[-1])
+            put(y, u, OFFS[c], WIDS[c], sem_pre.at[c, u])
+    for c in range(NLATE):
+        rbps[c][...] = rbs[c][...].reshape(N * KB, WIDS[NPRE + c])
     for u in range(ROWS // TM):
         m = pl.ds(u * TM, TM)
-
-        @pl.loop(0, WIDS[-1] // TN)
-        def _(t):
-            n = pl.ds(pl.multiple_of(t * TN, TN), TN)
-            ybuf[m, n] = product(hp_ref, ra, rbp, m, n)
-
-        put(ybuf, u, NCH - 1, sem.at[u])
+        for c in range(NLATE):
+            for t in range(WIDS[NPRE + c] // TN):
+                n = pl.ds(t * TN, TN)
+                o = pl.ds(OFFS[NPRE + c] - OFFS[NPRE] + t * TN, TN)
+                ybuf[m, o] = product(hp_ref, ras[c], rbps[c], m, n)
+        put(ybuf, u, OFFS[NPRE], COLS - OFFS[NPRE], sem.at[u])
     for copy in copies:
         copy.wait()
 
@@ -219,31 +223,33 @@
     any_, vmem = pl.BlockSpec(memory_space=pl.ANY), pl.BlockSpec(memory_space=pltpu.VMEM)
     hbm = pl.BlockSpec(memory_space=pltpu.HBM)
     dma = pltpu.SemaphoreType.DMA
-    last = WIDS[-1]
+    pre, late = WIDS[:NPRE], WIDS[NPRE:]
     passed = pl.pallas_call(
         exchange,
-        out_shape=(*[pltpu.VMEM((ROWS, wid), bf) for wid in WIDS[:NPRE]], pltpu.VMEM((ROWS, D), bf),
-                   pltpu.VMEM((N * KA, last), bf), pltpu.VMEM((N, KB, last), bf)),
+        out_shape=(*[pltpu.VMEM((ROWS, wid), bf) for wid in pre], pltpu.VMEM((ROWS, D), bf),
+                   *[pltpu.VMEM((N * KA, wid), bf) for wid in late], *[pltpu.VMEM((N, KB, wid), bf) for wid in late]),
         in_specs=[hbm, hbm],
-        out_specs=(vmem,) * (NPRE + 3),
+        out_specs=(vmem,) * (NPRE + 1 + 2 * NLATE),
         scratch_shapes=[
-            *[pltpu.VMEM((N * KA, wid), bf) for wid in WIDS[:NPRE]],
-            *[pltpu.VMEM((N, KB, wid), bf) for wid in WIDS[:NPRE]],
-            *[pltpu.VMEM((N * KB, wid), bf) for wid in WIDS[:NPRE]],
+            *[pltpu.VMEM((N * KA, wid), bf) for wid in pre],
+            *[pltpu.VMEM((N, KB, wid), bf) for wid in pre],
+            *[pltpu.VMEM((N * KB, wid), bf) for wid in pre],
             pltpu.VMEM((NP, NZ, BLK, D), bf), pltpu.VMEM((KB, N * COLS), bf),
-            pltpu.SemaphoreType.REGULAR((4,)), dma((2,)), dma, dma, dma, dma, dma, dma((NCH,)), dma((NCH,)), dma((NCH,)), dma((NCH,)),
+            pltpu.SemaphoreType.REGULAR((4,)), dma((2,)), dma, dma, dma, dma, dma,
+            dma((NCH,)), dma((NCH,)), dma((NCH,)), dma((NCH,)),
         ],
         compiler_params=pltpu.CompilerParams(
-            collective_id=0, has_side_effects=True, vmem_limit_bytes=22 * 2**20),
+            collective_id=0, has_side_effects=True, vmem_limit_bytes=19 * 2**20),
         name="exchange",
     )(pltpu.with_memory_space_constraint(h, pltpu.HBM), w)
     return pl.pallas_call(
         finish,
         out_shape=jax.ShapeDtypeStruct((ROWS, COLS), bf),
-        in_specs=[vmem] * (NPRE + 3),
+        in_specs=[vmem] * (NPRE + 1 + 2 * NLATE),
         out_specs=any_,
-        scratch_shapes=[pltpu.VMEM((N * KB, last), bf), pltpu.VMEM((ROWS, last), bf), dma((NPRE, ROWS // TM)), dma((ROWS // TM,))],
-        compiler_params=pltpu.CompilerParams(vmem_limit_bytes=22 * 2**20),
+        scratch_shapes=[*[pltpu.VMEM((N * KB, wid), bf) for wid in late], pltpu.VMEM((ROWS, sum(late)), bf),
+                        dma((NPRE, ROWS // TM)), dma((ROWS // TM,))],
+        compiler_params=pltpu.CompilerParams(vmem_limit_bytes=19 * 2**20),
         name="finish",
     )(*passed)
 

time: 248 us -> 253 us (1.020)
  Pallas kernels: 246 us -> 253 us
    pallas_call x1, Pallas kernels: 235 us -> 242 us  [local_part(): pl.pallas_call(exchange, out_shape=(*[pltpu.VMEM((ROWS, wid), bf) for wid...]
where the time goes in v7:
time: 253 us
  Pallas kernels  253 us (100%)
    pallas_call x1, Pallas kernels, local_part(): pl.pallas_call(exchange, out_shape=(*[pltpu.VMEM((ROWS, wid), bf) for wid...  242 us
    pallas_call x1, Pallas kernels, local_part(): pl.pallas_call(finish, out_shape=jax.ShapeDtypeStruct((ROWS, COLS), bf),...  11.1 us

profile of v7, /device:TPU:0, one launch (start us, length us, event | category | flops | bytes accessed | tf_op | source)
XLA Modules:
  0.0 253.1 jit_solution(6984591349007166745)
XLA Ops:
  0.0 241.9 %exchange.1 = (bf16[2048,2304]{1,0:T(8,128)(2,1)S(1)}, bf16[2048,2048]{1,0:T(8,128)(2,1)S(1)}, bf16[2048,1536]{1,0:T(8,128)(2,1)S(1)}, bf16[2048,1024]{1,0:T(8,1...) custom-call(bf16[64,640]{1,0:T(8,128)(2,1)} %h_ref.1, ...), custom_call_target="tpu_custom_call" | custom-call | tf_op jit(solution)/shard_map/exchange/pallas_call | solution.py:227
  241.9 11.1 %finish.1 = bf16[2048,8192]{1,0:T(8,128)(2,1)} custom-call(bf16[2048,2304]{1,0:T(8,128)(2,1)S(1)} %get-tuple-element.15.refs_0_, bf16[2048,2048]{1,0:T(8,128)(2,1)S(1)} %get-tuple-element.16.refs_1_, bf16[2048,1536]{1,0:T(8,128)(2,1)S(1)} %get-tuple-element.17.refs_2_, bf16[2048,1024]{1,0:T(8,128)(2,1)S(1)} %get-tuple-element.18.refs_3_, ...), custom_call_target="tpu_custom_call" | custom-call | tf_op jit(solution)/shard_map/finish/pallas_call | solution.py:245

commit v8 on v6

--- a/solution.py
+++ b/solution.py
@@ -12,7 +12,7 @@
 KA = 16
 KB = 4
 COLS = 8192
-WIDS = (2560, 2560, 2048, 1024)
+WIDS = (3328, 3328, 1536)
 OFFS = tuple(sum(WIDS[:c]) for c in range(len(WIDS)))
 NCH = len(WIDS)
 NPRE = NCH - 1
@@ -36,10 +36,10 @@
 
 
 def exchange(h_ref, w_ref, *refs):
-    ys, (hp_ref, ra_last, rb_last), refs = refs[:NPRE], refs[NPRE : NPRE + 3], refs[NPRE + 3 :]
-    ras, rbs, rbps, refs = refs[:NPRE], refs[NPRE : 2 * NPRE], refs[2 * NPRE : 3 * NPRE], refs[3 * NPRE :]
+    ys, (hp_ref, ra_last, rb), refs = refs[:NPRE], refs[NPRE : NPRE + 3], refs[NPRE + 3 :]
+    ras, rbps, refs = refs[:NPRE], refs[NPRE : 2 * NPRE], refs[2 * NPRE :]
     hraw, bsrc, news, loc, hz_s, hm_r, hn_r, hp_s, hp_r, a_s, a_r, b_s, b_r = refs
-    ras, rbs = (*ras, ra_last), (*rbs, rb_last)
+    ras = (*ras, ra_last)
     i, j = lax.axis_index("dp"), lax.axis_index("tp")
     me = i * NP + j
     inner = jnp.logical_and(i >= 1, i <= 2)
@@ -81,14 +81,16 @@
         dev = (i ^ kz) * NP + (j ^ kp)
         remote(w_ref.at[0:KA, cols(dev, c)], ras[c].at[rows_a, :], a_s.at[c], a_r.at[c], peer(kz, kp)).start()
 
-    def send_b(c, kz, kp):
+    def send_b(kz, kp):
         dev = (i ^ kz) * NP + (j ^ kp)
-        remote(bsrc.at[:, cols(dev, c)], rbs[c].at[me], b_s.at[c], b_r.at[c], peer(kz, kp)).start()
+        part = bsrc.at[:, pl.ds(pl.multiple_of(dev * COLS, COLS), COLS)]
+        remote(part, rb.at[me], b_s, b_r, peer(kz, kp)).start()
 
     def send_list(c, order):
         for kz, kp in order:
             send_a(c, kz, kp)
-            send_b(c, kz, kp)
+            if c == 0:
+                send_b(kz, kp)
 
     def send(c):
         @pl.when(inner)
@@ -103,7 +105,9 @@
 
     def own(c):
         pltpu.make_async_copy(w_ref.at[0:KA, cols(me, c)], ras[c].at[rows_a, :], a_r.at[c]).start()
-        pltpu.make_async_copy(w_ref.at[KA : KA + KB, cols(me, c)], rbs[c].at[me], b_r.at[c]).start()
+        if c == 0:
+            mine = pl.ds(pl.multiple_of(me * COLS, COLS), COLS)
+            pltpu.make_async_copy(w_ref.at[KA : KA + KB, mine], rb.at[me], b_r).start()
 
     def hidden(kz, r):
         remote(h_ref, hraw.at[j, i], hz_s, r, peer(kz, 0)).start()
@@ -114,8 +118,7 @@
         for c in range(LOOK):
             send_a(c, 3, 0)
         bcopy.wait()
-        for c in range(LOOK):
-            send_b(c, 3, 0)
+        send_b(3, 0)
         pl.semaphore_wait(news.at[1], 1)
         tell(news.at[2], 3)
         hidden(1, hn_r)
@@ -163,11 +166,12 @@
 
     for c in range(NCH):
         pltpu.make_async_copy(ras[c], ras[c], a_r.at[c]).wait()
-        pltpu.make_async_copy(rbs[c], rbs[c], b_r.at[c]).wait()
+        if c == 0:
+            pltpu.make_async_copy(rb, rb, b_r).wait()
         if c + LOOK < NCH:
             send(c + LOOK)
         if c < NPRE:
-            rbps[c][...] = rbs[c][...].reshape(N * KB, WIDS[c])
+            rbps[c][...] = rb[:, :, OFFS[c] : OFFS[c] + WIDS[c]].reshape(N * KB, WIDS[c])
 
             @pl.loop(0, WIDS[c] // TN)
             def _(t):
@@ -183,8 +187,8 @@
     for c in range(NCH):
         part = ras[c].at[0 : (N - 1) * KA, :]
         pltpu.make_async_copy(part, part, a_s.at[c]).wait()
-        part = rbs[c].at[0 : N - 1]
-        pltpu.make_async_copy(part, part, b_s.at[c]).wait()
+    part = rb.at[0 : N - 1]
+    pltpu.make_async_copy(part, part, b_s).wait()
 
 
 def finish(*refs):
@@ -200,7 +204,7 @@
     for u in range(ROWS // TM):
         for c, y in enumerate(ys):
             put(y, u, c, sem_pre.at[c, u])
-    rbp[...] = rb[...].reshape(N * KB, WIDS[-1])
+    rbp[...] = rb[:, :, OFFS[-1] :].reshape(N * KB, WIDS[-1])
     for u in range(ROWS // TM):
         m = pl.ds(u * TM, TM)
 
@@ -223,18 +227,17 @@
     passed = pl.pallas_call(
         exchange,
         out_shape=(*[pltpu.VMEM((ROWS, wid), bf) for wid in WIDS[:NPRE]], pltpu.VMEM((ROWS, D), bf),
-                   pltpu.VMEM((N * KA, last), bf), pltpu.VMEM((N, KB, last), bf)),
+                   pltpu.VMEM((N * KA, last), bf), pltpu.VMEM((N, KB, COLS), bf)),
         in_specs=[hbm, hbm],
         out_specs=(vmem,) * (NPRE + 3),
         scratch_shapes=[
             *[pltpu.VMEM((N * KA, wid), bf) for wid in WIDS[:NPRE]],
-            *[pltpu.VMEM((N, KB, wid), bf) for wid in WIDS[:NPRE]],
             *[pltpu.VMEM((N * KB, wid), bf) for wid in WIDS[:NPRE]],
             pltpu.VMEM((NP, NZ, BLK, D), bf), pltpu.VMEM((KB, N * COLS), bf),
-            pltpu.SemaphoreType.REGULAR((4,)), dma((2,)), dma, dma, dma, dma, dma, dma((NCH,)), dma((NCH,)), dma((NCH,)), dma((NCH,)),
+            pltpu.SemaphoreType.REGULAR((4,)), dma((2,)), dma, dma, dma, dma, dma, dma((NCH,)), dma((NCH,)), dma, dma,
         ],
         compiler_params=pltpu.CompilerParams(
-            collective_id=0, has_side_effects=True, vmem_limit_bytes=22 * 2**20),
+            collective_id=0, has_side_effects=True, vmem_limit_bytes=19 * 2**20),
         name="exchange",
     )(pltpu.with_memory_space_constraint(h, pltpu.HBM), w)
     return pl.pallas_call(
@@ -243,7 +246,7 @@
         in_specs=[vmem] * (NPRE + 3),
         out_specs=any_,
         scratch_shapes=[pltpu.VMEM((N * KB, last), bf), pltpu.VMEM((ROWS, last), bf), dma((NPRE, ROWS // TM)), dma((ROWS // TM,))],
-        compiler_params=pltpu.CompilerParams(vmem_limit_bytes=22 * 2**20),
+        compiler_params=pltpu.CompilerParams(vmem_limit_bytes=19 * 2**20),
         name="finish",
     )(*passed)
 

time: 248 us -> 262 us (1.056)
  Pallas kernels: 246 us -> 260 us
    pallas_call x1, Pallas kernels: 235 us -> 249 us  [local_part(): pl.pallas_call(exchange, out_shape=(*[pltpu.VMEM((ROWS, wid), bf) for wid...]
where the time goes in v8:
time: 262 us; the launch traced here: 260 us
  Pallas kernels  260 us (99%)
    pallas_call x1, Pallas kernels, local_part(): pl.pallas_call(exchange, out_shape=(*[pltpu.VMEM((ROWS, wid), bf) for wid...  249 us
    pallas_call x1, Pallas kernels, local_part(): pl.pallas_call(finish, out_shape=jax.ShapeDtypeStruct((ROWS, COLS), bf),...  11.1 us

profile of v8, /device:TPU:0, one launch (start us, length us, event | category | flops | bytes accessed | tf_op | source)
XLA Modules:
  0.0 260.0 jit_solution(10553610484021390668)
XLA Ops:
  0.0 248.9 %exchange.1 = (bf16[2048,3328]{1,0:T(8,128)(2,1)S(1)}, bf16[2048,3328]{1,0:T(8,128)(2,1)S(1)}, bf16[2048,640]{1,0:T(8,128)(2,1)S(1)}, bf16[512,1536]{1,0:T(8,128)(2,1)S(1)}, bf16[32,4,8192]{2,1,0:T(4,128)(2,1)S(1)}) custom-call(bf16[64,640]{1,0:T(8,128)(2,1)} %h_ref.1, bf16[20,262144]{1,0:T(8,128)(2,1)} %w_ref.1), custom_call_target="tpu_custom_call" | custom-call | tf_op jit(solution)/shard_map/exchange/pallas_call | solution.py:227
  248.9 11.1 %finish.1 = bf16[2048,8192]{1,0:T(8,128)(2,1)} custom-call(bf16[2048,3328]{1,0:T(8,128)(2,1)S(1)} %get-tuple-element.10.refs_0_, bf16[2048,3328]{1,0:T(8,128)(2,1)S(1)} %get-tuple-element.11.refs_1_, bf16[2048,640]{1,0:T(8,128)(2,1)S(1)} %get-tuple-element.12.refs_2_, bf16[512,1536]{1,0:T(8,128)(2,1)S(1)} %get-tuple-element.13.refs_3_, ...), custom_call_target="tpu_custom_call" | custom-call | tf_op jit(solution)/shard_map/finish/pallas_call | solution.py:243

commit v9 on v6

--- a/solution.py
+++ b/solution.py
@@ -16,13 +16,14 @@
 OFFS = tuple(sum(WIDS[:c]) for c in range(len(WIDS)))
 NCH = len(WIDS)
 NPRE = NCH - 1
-LOOK = 3
+LOOK = 2
+AHEAD = 3
 TN = 256
 TM = 512
 
 MSEQ = (0, 2, 4, 3, 1, 6, 5, 7)
-CROSS = [(kz, m) for m in MSEQ for kz in (2, 3)]
-STAY = [(kz, m) for m in MSEQ for kz in (1, 0) if (kz, m) != (0, 0)]
+ORDER = [(kz, m) for m in range(NP) for kz in (2, 1, 3, 0) if (kz, m) != (0, 0)]
+EARLY = [(0, 2), (0, 4), (0, 3), (0, 1), (1, 0)]
 
 
 def plane(kz):
@@ -91,13 +92,16 @@
             send_b(c, kz, kp)
 
     def send(c):
-        @pl.when(inner)
-        def _():
-            send_list(c, [k for k in CROSS if c >= LOOK or k != (3, 0)] + STAY)
-
-        @pl.when(jnp.logical_not(inner))
-        def _():
-            send_list(c, STAY + CROSS)
+        if c < AHEAD:
+            @pl.when(inner)
+            def _():
+                send_list(c, [k for k in ORDER if k != (3, 0)])
+
+            @pl.when(jnp.logical_not(inner))
+            def _():
+                send_list(c, ORDER)
+        else:
+            send_list(c, ORDER)
 
         own(c)
 
@@ -111,17 +115,17 @@
     @pl.when(inner)
     def _():
         hidden(3, hm_r)
-        for c in range(LOOK):
+        for c in range(AHEAD):
             send_a(c, 3, 0)
         bcopy.wait()
-        for c in range(LOOK):
+        for c in range(AHEAD):
             send_b(c, 3, 0)
         pl.semaphore_wait(news.at[1], 1)
         tell(news.at[2], 3)
         hidden(1, hn_r)
         pl.semaphore_wait(news.at[2], 1)
         tell(news.at[3], 1)
-        send_list(0, plane(3)[1:] + plane(2) + STAY)
+        send_list(0, [k for k in ORDER if k != (3, 0)])
 
     @pl.when(jnp.logical_not(inner))
     def _():
@@ -129,13 +133,13 @@
             tell(news.at[0], kz, kp)
         hidden(1, hn_r)
         bcopy.wait()
-        send_list(0, plane(0))
+        send_list(0, EARLY[:4])
         pl.semaphore_wait(news.at[0], NP - 1)
         tell(news.at[1], 1)
-        send_list(0, plane(1))
+        send_list(0, EARLY[4:])
         pl.semaphore_wait(news.at[3], 1)
         hidden(3, hm_r)
-        send_list(0, CROSS)
+        send_list(0, [k for k in ORDER if k not in EARLY])
 
     own(0)
     got = hraw.at[j, NZ - 1 - i]
@@ -234,7 +238,7 @@
             pltpu.SemaphoreType.REGULAR((4,)), dma((2,)), dma, dma, dma, dma, dma, dma((NCH,)), dma((NCH,)), dma((NCH,)), dma((NCH,)),
         ],
         compiler_params=pltpu.CompilerParams(
-            collective_id=0, has_side_effects=True, vmem_limit_bytes=22 * 2**20),
+            collective_id=0, has_side_effects=True, vmem_limit_bytes=19 * 2**20),
         name="exchange",
     )(pltpu.with_memory_space_constraint(h, pltpu.HBM), w)
     return pl.pallas_call(
@@ -243,7 +247,7 @@
         in_specs=[vmem] * (NPRE + 3),
         out_specs=any_,
         scratch_shapes=[pltpu.VMEM((N * KB, last), bf), pltpu.VMEM((ROWS, last), bf), dma((NPRE, ROWS // TM)), dma((ROWS // TM,))],
-        compiler_params=pltpu.CompilerParams(vmem_limit_bytes=22 * 2**20),
+        compiler_params=pltpu.CompilerParams(vmem_limit_bytes=19 * 2**20),
         name="finish",
     )(*passed)
 

time: 248 us -> 247 us (level)
  no operation moved by 1% of the time
where the time goes in v9:
time: 247 us
  Pallas kernels  247 us (100%)
    pallas_call x1, Pallas kernels, local_part(): pl.pallas_call(exchange, out_shape=(*[pltpu.VMEM((ROWS, wid), bf) for wid...  236 us
    pallas_call x1, Pallas kernels, local_part(): pl.pallas_call(finish, out_shape=jax.ShapeDtypeStruct((ROWS, COLS), bf),...  11 us

profile of v9, /device:TPU:0, one launch (start us, length us, event | category | flops | bytes accessed | tf_op | source)
XLA Modules:
  0.0 246.8 jit_solution(16340139632602996069)
XLA Ops:
  0.0 235.8 %exchange.1 = (bf16[2048,2560]{1,0:T(8,128)(2,1)S(1)}, bf16[2048,2560]{1,0:T(8,128)(2,1)S(1)}, bf16[2048,2048]{1,0:T(8,128)(2,1)S(1)}, bf16[2048,640]{1,0:T(8,12...) custom-call(bf16[64,640]{1,0:T(8,128)(2,1)} %h_ref.1, bf16[20,262144]{1,0:T(8,128)(2,1)} %w_ref.1), custom_call_target="tpu_custom_call" | custom-call | tf_op jit(solution)/shard_map/exchange/pallas_call | solution.py:227
  235.8 11.0 %finish.1 = bf16[2048,8192]{1,0:T(8,128)(2,1)} custom-call(bf16[2048,2560]{1,0:T(8,128)(2,1)S(1)} %get-tuple-element.11.refs_0_, bf16[2048,2560]{1,0:T(8,128)(2,1)S(1)} %get-tuple-element.12.refs_1_, bf16[2048,2048]{1,0:T(8,128)(2,1)S(1)} %get-tuple-element.13.refs_2_, bf16[2048,640]{1,0:T(8,128)(2,1)S(1)} %get-tuple-element.14.refs_3_, ...), custom_call_target="tpu_custom_call" | custom-call | tf_op jit(solution)/shard_map/finish/pallas_call | solution.py:244

commit v10 on v9

--- a/solution.py
+++ b/solution.py
@@ -12,7 +12,7 @@
 KA = 16
 KB = 4
 COLS = 8192
-WIDS = (2560, 2560, 2048, 1024)
+WIDS = (2304, 2304, 2048, 1536)
 OFFS = tuple(sum(WIDS[:c]) for c in range(len(WIDS)))
 NCH = len(WIDS)
 NPRE = NCH - 1

time: 247 us -> 249 us (level)
  no operation moved by 1% of the time
where the time goes in v10:
time: 249 us; the launch traced here: 247 us
  Pallas kernels  247 us (99%)
    pallas_call x1, Pallas kernels, local_part(): pl.pallas_call(exchange, out_shape=(*[pltpu.VMEM((ROWS, wid), bf) for wid...  236 us
    pallas_call x1, Pallas kernels, local_part(): pl.pallas_call(finish, out_shape=jax.ShapeDtypeStruct((ROWS, COLS), bf),...  11 us

profile of v10, /device:TPU:0, one launch (start us, length us, event | category | flops | bytes accessed | tf_op | source)
XLA Modules:
  0.0 247.3 jit_solution(15107312465367532795)
XLA Ops:
  0.0 236.3 %exchange.1 = (bf16[2048,2304]{1,0:T(8,128)(2,1)S(1)}, bf16[2048,2304]{1,0:T(8,128)(2,1)S(1)}, bf16[2048,2048]{1,0:T(8,128)(2,1)S(1)}, bf16[2048,640]{1,0:T(8,12...) custom-call(bf16[64,640]{1,0:T(8,128)(2,1)} %h_ref.1, bf16[20,262144]{1,0:T(8,128)(2,1)} %w_ref.1), custom_call_target="tpu_custom_call" | custom-call | tf_op jit(solution)/shard_map/exchange/pallas_call | solution.py:227
  236.3 11.0 %finish.1 = bf16[2048,8192]{1,0:T(8,128)(2,1)} custom-call(bf16[2048,2304]{1,0:T(8,128)(2,1)S(1)} %get-tuple-element.11.refs_0_, bf16[2048,2304]{1,0:T(8,128)(2,1)S(1)} %get-tuple-element.12.refs_1_, bf16[2048,2048]{1,0:T(8,128)(2,1)S(1)} %get-tuple-element.13.refs_2_, bf16[2048,640]{1,0:T(8,128)(2,1)S(1)} %get-tuple-element.14.refs_3_, ...), custom_call_target="tpu_custom_call" | custom-call | tf_op jit(solution)/shard_map/finish/pallas_call | solution.py:244
